TPU v7x, 32 devices: a whole 2x2x4 slice. The times are simulated.
32 devices in a mesh: gx: 2 (over x), gy: 4 (over y, core), gz: 4 (over z).
Axes of the slice: x: 2, y: 2, z: 4, core: 2. Of those that a mesh axis runs over, the one named last changes fastest.
Arguments:
- features: bfloat16 [256, 4096], P('gz', ('gy', 'gx')), may hold values from -14 to 14, as said below
- tiles: bfloat16 [32, 32, 128, 128], P('gx', 'gy'), may hold values from -0.5 to 0.5
- block_mask: int32 [32, 32], P('gx', 'gy'), may hold values from 0 to 1, as said below
- tile_counts: int32 [32], P('gx'), may hold values from 1 to 32, as said below
- weight: bfloat16 [256, 256], replicated, may hold values from -0.375 to 0.375
- gamma: float32 [256], P('gz'), may hold values from 0.5 to 2
- beta: float32 [256], P('gz'), may hold values from -3 to 3
Outputs:
- normed: bfloat16 [256, 4096], P('gz', ('gx', 'gy'))
Inputs may be any that keep to these rules, and one draw needn't show every extreme that they name: `features`: channels along dimension 0, nodes along dimension 1. `block_mask`: 1 where block row and block column meet in a nonzero block, else 0; the diagonal is 1. tile_counts[r] is the number of ones in row r of block_mask.
All inputs are finite; a program needn't handle non-finite values.
Results may differ from a plain program's by a relative error of at most 0.013.
Values may be sent and summed in bfloat16 or wider, within the bound.
A program may use at most 64 MiB of HBM per device.

v0:
```python
import jax
import jax.numpy as jnp
from jax import lax
from jax.sharding import PartitionSpec as P


def body(features, tiles, block_mask, tile_counts, weight, gamma, beta):
    panel = lax.all_gather(features, "gx", axis=1, tiled=True)
    local_ch = panel.shape[0]
    rows_blk = tiles.shape[0]
    cols_blk = tiles.shape[1]
    tile_len = tiles.shape[2]
    panels = panel.reshape(local_ch, cols_blk, tile_len)
    prods = jnp.einsum("fcn,rcmn->frcm", panels, tiles, preferred_element_type=jnp.float32)
    share = block_mask.astype(jnp.float32) / tile_counts.astype(jnp.float32)[:, None]
    partial_value = jnp.einsum("frcm,rc->frm", prods, share).reshape(local_ch, rows_blk * tile_len)
    summed = lax.psum(partial_value, "gy")
    width = rows_blk * tile_len // lax.axis_size("gy")
    agg = lax.dynamic_slice_in_dim(summed, lax.axis_index("gy") * width, width, 1)
    agg = agg.astype(jnp.bfloat16)
    offset = lax.axis_index("gz") * local_ch
    full = lax.all_gather(agg, "gz", axis=0, tiled=True)
    w_cols = lax.dynamic_slice_in_dim(weight, offset, local_ch, 1)
    z_vals = jnp.einsum("co,cn->on", w_cols, full, preferred_element_type=jnp.float32)
    total = z_vals.shape[1] * lax.axis_size(("gx", "gy"))
    sums, squares = lax.psum(
        (jnp.sum(z_vals, axis=1), jnp.sum(z_vals * z_vals, axis=1)), ("gx", "gy")
    )
    mean = sums / total
    var = squares / total - mean * mean
    centered = z_vals - mean[:, None]
    scaled = gamma[:, None] * centered * lax.rsqrt(var + 1e-05)[:, None] + beta[:, None]
    return jnp.maximum(scaled, 0.0).astype(jnp.bfloat16)


def solution(mesh):
    in_specs = (
        P("gz", ("gy", "gx")),
        P("gx", "gy", None, None),
        P("gx", "gy"),
        P("gx"),
        P(),
        P("gz"),
        P("gz"),
    )
    out_specs = P("gz", ("gx", "gy"))
    return jax.shard_map(body, mesh=mesh, in_specs=in_specs, out_specs=out_specs, check_vma=False)
```

profile of v0, /device:TPU:0, one launch (start us, length us, event | category | flops | bytes accessed | tf_op | source)
XLA Modules:
  0.0 57.3 jit_solution(9171550169248883873)
XLA Ops:
  0.0 0.0 copy-start
  0.0 0.7 %convert_element_type.13 = f32[16]{0:T(128)S(1)} convert(s32[16]{0:T(128)} %param.10) | non-fusion elementwise | flops 16 | bytes 128 | tf_op jit(solution)/shard_map/convert_element_type | solution.py:15
  0.7 0.7 %divide_bitcast_fusion = bf16[16,8,1,1]{0,1,2,3:T(8,128)(2,1)S(1)} fusion(s32[16,8]{0,1:T(8,128)} %param.9, f32[16]{0:T(128)S(1)} %convert_element_type.13), kind=kLoop, calls=%fused_computation.12 | loop fusion | flops 384 | bytes 832 | tf_op jit(solution)/shard_map/div | solution.py:15
  1.4 0.1 copy.12
  1.5 6.1 %all_gather.6 = bf16[64,1024]{1,0:T(8,128)(2,1)S(1)} all-gather(bf16[64,512]{1,0:T(8,128)(2,1)} %param.7), channel_id=1, replica_groups=mesh['gx'=2,'gy'=4,'gz'=4] {'gx'}, dimensions={1}, use_global_device_ids=true | all-gather | bytes 196608 | tf_op jit(solution)/shard_map/all_gather | solution.py:8
  7.6 3.8 %fusion.4 = bf16[64,16,8,128]{3,0,1,2:T(8,128)(2,1)S(1)} fusion(bf16[16,8,128,128]{3,2,1,0:T(8,128)(2,1)} %param.8, bf16[64,8,128,1]{2,1,0,3:T(8,128)(2,1)S(1)} %bitcast.19), kind=kOutput, calls=%fused_computation.4 | convolution fusion | flops 268435456 | bytes 6422528 | tf_op jit(solution)/shard_map/fcn,rcmn->frcm/dot_general | solution.py:14
  11.4 1.4 %fusion = f32[16,1,64,128]{3,1,2,0:T(1,128)S(1)} fusion(bf16[16,8,1,1]{1,2,3,0:T(2,128)(2,1)S(1)} %copy.12, bf16[64,16,8,128]{3,0,1,2:T(8,128)(2,1)S(1)} %fusion.4), kind=kOutput, calls=%fused_computation | convolution fusion | flops 2097152 | bytes 2621696 | tf_op jit(solution)/shard_map/frcm,rc->frm/dot_general | solution.py:16
  12.8 0.0 copy-start.1
  12.8 0.0 copy-start.2
  12.8 0.3 copy.14
  13.2 0.2 copy.28
  13.3 16.7 %all-reduce.2 = bf16[64,2048]{1,0:T(8,128)(2,1)S(1)} all-reduce(f32[64,2048]{1,0:T(8,128)S(1)} %bitcast.18), channel_id=1, replica_groups=mesh['gx'=2,'gy'=4,'gz'=4] {'gy'}, use_global_device_ids=true, to_apply=%region_0.0 | all-reduce | flops 131072 | bytes 786432 | tf_op jit(solution)/shard_map/psum | solution.py:17
  30.1 14.2 %all_gather.7 = bf16[256,512]{1,0:T(8,128)(2,1)S(1)} all-gather(bf16[64,512]{1,0:T(8,128)(2,1)S(1)} %dynamic-slice_convert_fusion), channel_id=1, replica_groups=mesh['gx'=2,'gy'=4,'gz'=4] {'gz'}, dimensions={0}, use_global_device_ids=true | all-gather | bytes 327680 | tf_op jit(solution)/shard_map/all_gather | solution.py:22
  44.3 0.0 copy-done
  44.3 0.4 fusion.11
  44.7 11.8 %all-reduce = (f32[64]{0:T(128)S(1)}, f32[64]{0:T(128)S(1)}) all-reduce(f32[64]{0:T(128)S(1)} %get-tuple-element.6, f32[64]{0:T(128)S(1)} %get-tuple-element.5), channel_id=1, replica_groups=mesh['gx'=2,'gy'=4,'gz'=4] {'gx','gy'}, use_global_device_ids=true, to_apply=%region_4.0 | all-reduce | flops 128 | bytes 1024 | tf_op jit(solution)/shard_map/psum | solution.py:26
  56.5 0.0 copy-done.1
  56.5 0.0 copy-done.2
  56.5 0.7 %maximum_convert_fusion = bf16[64,512]{1,0:T(8,128)(2,1)} fusion(f32[64,512]{1,0:T(8,128)S(1)} %get-tuple-element.11, f32[64]{0:T(128)S(1)} %copy-done.1, f32[64]{0:T(128)S(1)} %get-tuple-element.10, f32[64]{0:T(128)S(1)} %get-tuple-element.9, f32[64]{0:T(128)S(1)} %copy-done.2), kind=kLoop, calls=%fused_computation.7 | loop fusion | flops 196608 | bytes 197632 | tf_op jit(solution)/shard_map/convert_element_type | solution.py:33
  (3 shorter events, 0.0 us)
Async XLA Ops:
  0.0 44.3 %copy-start = (bf16[256,256]{1,0:T(8,128)(2,1)S(1)}, bf16[256,256]{1,0:T(8,128)(2,1)}, u32[]{:S(2)}) copy-start(bf16[256,256]{1,0:T(8,128)(2,1)} %param.11) | copy-start | bytes 393220
  12.8 43.7 %copy-start.1 = (f32[64]{0:T(128)S(1)}, f32[64]{0:T(128)}, u32[]{:S(2)}) copy-start(f32[64]{0:T(128)} %param.13) | copy-start | bytes 772
  12.8 43.7 %copy-start.2 = (f32[64]{0:T(128)S(1)}, f32[64]{0:T(128)}, u32[]{:S(2)}) copy-start(f32[64]{0:T(128)} %param.12) | copy-start | bytes 772
where the time goes:
time: 57.5 us; the launch traced here: 57.3 us
  blocking collectives  48.9 us (85%)
  matrix products  5.54 us (10%)
  other arithmetic  2.13 us (4%)
  local copies, waits for them, and re-layouts  0.61 us (1%)
    psum x1, blocking collectives, body(): summed = lax.psum(partial_value, 'gy')  16.7 us
    all_gather x1, blocking collectives, body(): full = lax.all_gather(agg, 'gz', axis=0, tiled=True)  14.2 us
    psum x1, blocking collectives, body(): lax.psum((jnp.sum(z_vals, axis=1), jnp.sum(z_vals * z_vals, axis=1)), ('g...  11.8 us
    all_gather x1, blocking collectives, body(): panel = lax.all_gather(features, 'gx', axis=1, tiled=True)  6.13 us
    dot_general x1, matrix products, body(): jnp.einsum('fcn,rcmn->frcm', panels, tiles, preferred_element_type=jnp.fl...  3.75 us
    dot_general x1, matrix products, body(): jnp.einsum('frcm,rc->frm', prods, share)  1.42 us

commit v1 on v0

--- a/solution.py
+++ b/solution.py
@@ -14,7 +14,7 @@
     prods = jnp.einsum("fcn,rcmn->frcm", panels, tiles, preferred_element_type=jnp.float32)
     share = block_mask.astype(jnp.float32) / tile_counts.astype(jnp.float32)[:, None]
     partial_value = jnp.einsum("frcm,rc->frm", prods, share).reshape(local_ch, rows_blk * tile_len)
-    summed = lax.psum(partial_value, "gy")
+    summed = jnp.sum(lax.all_gather(partial_value, "gy"), axis=0)
     width = rows_blk * tile_len // lax.axis_size("gy")
     agg = lax.dynamic_slice_in_dim(summed, lax.axis_index("gy") * width, width, 1)
     agg = agg.astype(jnp.bfloat16)

time: 57.5 us -> 80.8 us (1.41)
  waiting for transfers between devices: 0 us -> 24.5 us
  blocking collectives: 48.9 us -> 31.9 us
  between operations: 0.07 us -> 13.4 us
  other arithmetic: 2.13 us -> 3.92 us
    all_gather x0 -> x1, waiting for transfers between devices: none -> 24.4 us  [body(): summed = jnp.sum(lax.all_gather(partial_value, 'gy'), axis=0)]
    psum x1 -> x0, blocking collectives: 16.7 us -> none  [body(): summed = lax.psum(partial_value, 'gy')]
    reduce_sum x0 -> x1, other arithmetic: none -> 1.79 us  [body(): summed = jnp.sum(lax.all_gather(partial_value, 'gy'), axis=0)]
    another operation x0 -> x1, local copies, waits for them, and re-layouts: none -> 0.88 us  [body(): summed = jnp.sum(lax.all_gather(partial_value, 'gy'), axis=0)]
  transfers between devices with their start and end apart: 0 -> 1, of which waited for: 0 -> 1; matrix products, arithmetic and copies ran while one was open for 0% -> 0% of each run, Pallas kernels for 0% -> 0%
where the time goes in v1:
time: 80.8 us; the launch traced here: 80.6 us
  blocking collectives  31.9 us (39%)
  waiting for transfers between devices  24.5 us (30%)
  between operations  13.4 us (17%)
  matrix products  5.54 us (7%)
  other arithmetic  3.92 us (5%)
  local copies, waits for them, and re-layouts  1.33 us (2%)
    all_gather x1, waiting for transfers between devices, body(): summed = jnp.sum(lax.all_gather(partial_value, 'gy'), axis=0)  24.4 us
    all_gather x1, blocking collectives, body(): full = lax.all_gather(agg, 'gz', axis=0, tiled=True)  13.9 us
    psum x1, blocking collectives, body(): lax.psum((jnp.sum(z_vals, axis=1), jnp.sum(z_vals * z_vals, axis=1)), ('g...  11.8 us
    all_gather x1, blocking collectives, body(): panel = lax.all_gather(features, 'gx', axis=1, tiled=True)  6.13 us
    dot_general x1, matrix products, body(): jnp.einsum('fcn,rcmn->frcm', panels, tiles, preferred_element_type=jnp.fl...  3.75 us
    reduce_sum x1, other arithmetic, body(): summed = jnp.sum(lax.all_gather(partial_value, 'gy'), axis=0)  1.79 us
  transfers between devices with their start and end apart: 1, of which 1 were waited for; matrix products, arithmetic and copies ran while one was open for 0% of the time, Pallas kernels for 0%

profile of v1, /device:TPU:0, one launch (start us, length us, event | category | flops | bytes accessed | tf_op | source)
XLA Modules:
  0.0 80.6 jit_solution(9903522646537438841)
XLA Ops:
  6.5 0.0 copy-start
  6.5 0.0 all-gather.2.cloned.1.call-start
  6.5 0.7 convert_element_type.13
  7.2 0.7 divide_bitcast_fusion
  7.9 0.1 copy.12
  8.0 6.1 %all_gather.9 = bf16[64,1024]{1,0:T(8,128)(2,1)S(1)} all-gather(bf16[64,512]{1,0:T(8,128)(2,1)} %param.7), channel_id=1, replica_groups=mesh['gx'=2,'gy'=4,'gz'=4] {'gx'}, dimensions={1}, use_global_device_ids=true | all-gather | bytes 196608 | tf_op jit(solution)/shard_map/all_gather | solution.py:8
  14.2 3.8 %fusion.4 = bf16[64,16,8,128]{3,0,1,2:T(8,128)(2,1)S(1)} fusion(bf16[16,8,128,128]{3,2,1,0:T(8,128)(2,1)} %param.8, bf16[64,8,128,1]{2,1,0,3:T(8,128)(2,1)S(1)} %bitcast.16), kind=kOutput, calls=%fused_computation.4 | convolution fusion | flops 268435456 | bytes 6422528 | tf_op jit(solution)/shard_map/fcn,rcmn->frcm/dot_general | solution.py:14
  17.9 1.4 %fusion = f32[16,1,64,128]{3,1,2,0:T(1,128)S(1)} fusion(bf16[16,8,1,1]{1,2,3,0:T(2,128)(2,1)S(1)} %copy.12, bf16[64,16,8,128]{3,0,1,2:T(8,128)(2,1)S(1)} %fusion.4), kind=kOutput, calls=%fused_computation | convolution fusion | flops 2097152 | bytes 2621696 | tf_op jit(solution)/shard_map/frcm,rc->frm/dot_general | solution.py:16
  19.4 0.3 copy.27
  19.7 0.9 %all_gather_reshape.3 = f32[1,64,2048]{2,1,0:T(8,128)} reshape(f32[64,16,128]{2,1,0:T(8,128)S(1)} %bitcast.15) | data formatting | bytes 1048576 | tf_op jit(solution)/shard_map/all_gather;reshape | solution.py:17
  20.5 0.0 copy-start.1
  20.6 0.0 copy-start.2
  20.6 0.0 all-gather.2.cloned.1.call-update
  20.6 24.4 %all-gather.2.cloned.1.call-done = f32[4,64,2048]{2,1,0:T(8,128)} async-done(((f32[1,64,2048]{2,1,0:T(8,128)}), f32[4,64,2048]{2,1,0:T(8,128)}) %all-gather.2.cloned.1.call-update) | async-done | bytes 2097168 | tf_op jit(solution)/shard_map/all_gather | solution.py:17
  45.0 1.8 %reduce_sum.27 = bf16[64,2048]{1,0:T(8,128)(2,1)S(1)} reduce(f32[4,64,2048]{2,1,0:T(8,128)} %all-gather.2.cloned.1.call-done, f32[]{:T(128)} %constant.8.clone.1), dimensions={0}, to_apply=%region_0.0 | reduce | flops 393216 | bytes 2359300 | tf_op jit(solution)/shard_map/reduce_sum | solution.py:17
  46.8 13.9 %all_gather.11 = bf16[256,512]{1,0:T(8,128)(2,1)S(1)} all-gather(bf16[64,512]{1,0:T(8,128)(2,1)S(1)} %dynamic-slice_convert_fusion), channel_id=1, replica_groups=mesh['gx'=2,'gy'=4,'gz'=4] {'gz'}, dimensions={0}, use_global_device_ids=true | all-gather | bytes 327680 | tf_op jit(solution)/shard_map/all_gather | solution.py:22
  60.8 0.0 copy-done
  60.8 0.4 fusion.11
  61.1 11.8 %all-reduce = (f32[64]{0:T(128)S(1)}, f32[64]{0:T(128)S(1)}) all-reduce(f32[64]{0:T(128)S(1)} %get-tuple-element.6, f32[64]{0:T(128)S(1)} %get-tuple-element.5), channel_id=1, replica_groups=mesh['gx'=2,'gy'=4,'gz'=4] {'gx','gy'}, use_global_device_ids=true, to_apply=%region_4.0 | all-reduce | flops 128 | bytes 1024 | tf_op jit(solution)/shard_map/psum | solution.py:26
  73.0 0.0 copy-done.1
  73.0 0.0 copy-done.2
  73.0 0.7 maximum_convert_fusion
  (3 shorter events, 0.0 us)
Async XLA Ops:
  6.5 54.2 %copy-start = (bf16[256,256]{1,0:T(8,128)(2,1)S(1)}, bf16[256,256]{1,0:T(8,128)(2,1)}, u32[]{:S(2)}) copy-start(bf16[256,256]{1,0:T(8,128)(2,1)} %param.11) | copy-start | bytes 393220
  6.5 38.5 %all-gather.2.cloned.1.call-start = ((), (), s32[]{:S(2)}) async-start(), calls=%async_computation | async-start | bytes 2621440 | tf_op jit(solution)/shard_map/all_gather | solution.py:17
  20.5 52.4 %copy-start.1 = (f32[64]{0:T(128)S(1)}, f32[64]{0:T(128)}, u32[]{:S(2)}) copy-start(f32[64]{0:T(128)} %param.13) | copy-start | bytes 772
  20.6 52.4 %copy-start.2 = (f32[64]{0:T(128)S(1)}, f32[64]{0:T(128)}, u32[]{:S(2)}) copy-start(f32[64]{0:T(128)} %param.12) | copy-start | bytes 772
Sparse Core Ops, SparseCore 0:
  20.7 24.2 all-gather.1
